TPU v7x, 32 devices: a whole 2x2x4 slice. The times are simulated.
32 devices in a mesh: feat: 8 (over y, x, core), rep: 4 (over z).
Axes of the slice: x: 2, y: 2, z: 4, core: 2. Of those that a mesh axis runs over, the one named last changes fastest.
Arguments:
- features: bfloat16 [4, 8, 1024, 512], P('rep', None, 'feat'), may hold values from -6 to 6
- adjacency_one: int32 [4, 8, 5, 16, 512], P('rep'), may hold values from 0 to 65535, as said below
- pre_hidden: bfloat16 [4, 8, 256, 256], P('rep', 'feat'), may hold values from -6 to 6
- adjacency_two: int32 [4, 8, 5, 8, 256], P('rep', 'feat'), may hold values from 0 to 65535, as said below
- weight_two: bfloat16 [6, 256, 256], replicated, may hold values from -0.375 to 0.375
- out_grad: bfloat16 [4, 8, 128, 256], P('rep', 'feat'), may hold values from -6 to 6
Outputs:
- grad_w1: float32 [6, 1024, 256], P(None, 'feat')
- grad_b1: float32 [256], replicated
- grad_w2: float32 [6, 256, 256], replicated
- grad_b2: float32 [256], replicated
Inputs may be any that keep to these rules, and one draw needn't show every extreme that they name: `adjacency_one`: bit k, k below 16, of word (w, n) is the entry of destination row 16 w + k and source column n; higher bits are zero; some rows are empty. `adjacency_two`: bit k, k below 16, of word (w, n) is the entry of seed row 16 w + k and source column n; higher bits are zero; some rows are empty.
All inputs are finite; a program needn't handle non-finite values.
Results may differ from a plain program's by a relative error of at most 0.0041.
Values may be sent and summed in bfloat16 or wider, within the bound.
A program may use at most 128 MiB of HBM per device.

v0:
```python
import functools

import jax
import jax.numpy as jnp
from jax import lax
from jax.experimental import pallas as pl
from jax.experimental.pallas import tpu as pltpu
from jax.sharding import PartitionSpec as P

F32 = jnp.float32
BF16 = jnp.bfloat16
MESH = pl.DeviceIdType.MESH
BITS = 16


def dot_nn(a, b):
    return lax.dot_general(a, b, (((1,), (0,)), ((), ())), preferred_element_type=F32)


def dot_nt(a, b):
    return lax.dot_general(a, b, (((1,), (1,)), ((), ())), preferred_element_type=F32)


def dot_tn(a, b):
    return lax.dot_general(a, b, (((0,), (0,)), ((), ())), preferred_element_type=F32)


def plane_order(rows):
    words = rows // BITS
    to = lax.broadcasted_iota(jnp.int32, (rows, rows), 0)
    source = lax.broadcasted_iota(jnp.int32, (rows, rows), 1)
    wanted = (to % words) * BITS + to // words
    return jnp.where(source == wanted, 1.0, 0.0).astype(BF16)


def remote(src, dst, send, recv, **where):
    return pltpu.make_async_remote_copy(
        src_ref=src, dst_ref=dst, send_sem=send, recv_sem=recv,
        device_id=where, device_id_type=MESH,
    )


def kernel(
    feats, reps, factor,
    x_hbm, words_hbm, pre_ref, words_two_ref, weight_hbm, grad_ref,
    out_one, out_two, out_bias,
    x_ref, words_ref, weight_ref, panels, hbuf, order_ref, acc_one, wire_one, land_one,
    flat_two, pair_two, wire_two, land_two, mine_two, send_two, rep_two, group_two,
    bias_pair, bias_feat, bias_rep,
    local_sem, h_send, h_fwd, h_recv,
    p_send, p_recv, s_send, s_recv, r_send, r_recv, z_send, z_recv, g_send, g_fwd, g_recv,
    a_send, a_recv, c_send, c_recv,
    bp_sem, bs_send, bs_recv, br_send, br_recv,
):
    me = lax.axis_index("feat")
    my_rep = lax.axis_index("rep")
    half = feats // 2
    parity = lax.rem(me, 2)
    mate = me + 1 - 2 * parity
    place = me // 2
    batches, columns, nodes = x_ref.shape
    relations, words_one = words_ref.shape[1], words_ref.shape[2]
    rows = words_one * BITS
    words_two = words_two_ref.shape[1]
    seeds = words_two * BITS
    hidden_width = pre_ref.shape[1]
    part_two = out_two.shape[2]
    share_two = reps * part_two
    share_one = out_one.shape[1]

    def peer(t):
        return lax.rem(me + 2 * t, feats)

    def rep_peer(t):
        return lax.rem(my_rep + t, reps)

    fetch_x = pltpu.make_async_copy(x_hbm, x_ref, local_sem.at[0])
    fetch_words = pltpu.make_async_copy(words_hbm, words_ref, local_sem.at[1])
    fetch_weight = pltpu.make_async_copy(weight_hbm, weight_ref, local_sem.at[2])
    fetch_weight.start()

    barrier = pltpu.get_barrier_semaphore()
    for t in range(1, half):
        pl.semaphore_signal(barrier, inc=1, device_id={"feat": peer(t)}, device_id_type=MESH)
    pl.semaphore_signal(barrier, inc=1, device_id={"feat": mate}, device_id_type=MESH)
    for t in range(1, reps):
        pl.semaphore_signal(barrier, inc=1, device_id={"rep": rep_peer(t)}, device_id_type=MESH)

    pre = pre_ref[...]
    hidden = jnp.maximum(pre, 0)
    scaled = grad_ref[...].astype(F32) * factor
    scaled_low = scaled.astype(BF16)
    scaled_plane = dot_nn(plane_order(seeds), scaled_low).astype(BF16)
    planes = []
    for r in range(relations):
        words = words_two_ref[r]
        for k in range(BITS):
            planes.append(jnp.bitwise_and(jnp.right_shift(words, k), 1).astype(F32))
    matrix_two = jnp.concatenate(planes, 0).astype(BF16)
    degree = dot_nn(matrix_two, jnp.ones((rows, hidden_width), BF16))
    inverse_two = 1.0 / jnp.maximum(degree, 1.0)
    fetch_weight.wait()
    fetch_x.start()
    fetch_words.start()
    backed = jnp.concatenate(
        [dot_nt(scaled_plane, weight_ref[r + 1]) for r in range(relations)], 0
    )
    backed = (backed * inverse_two).astype(BF16)
    total = dot_tn(matrix_two, backed)
    own = dot_nt(scaled_low, weight_ref[0])
    total = jnp.concatenate([total[:seeds] + own, total[seeds:]], 0)
    hidden_grad = jnp.where(pre.astype(F32) > 0, total, 0.0).astype(BF16)
    order = plane_order(rows)
    order_ref[...] = order
    hbuf[me] = dot_nn(order, hidden_grad).astype(BF16)

    pl.semaphore_wait(barrier, half + reps - 1)
    pending = []

    def go(copy):
        copy.start()
        pending.append(copy)

    for t in range(1, half):
        go(remote(hbuf.at[me], hbuf.at[me], h_send.at[t], h_recv.at[me], feat=peer(t)))
    go(remote(hbuf.at[me], hbuf.at[me], h_send.at[0], h_recv.at[me], feat=mate))

    sum_one = jnp.sum(hidden_grad.astype(F32), 0, keepdims=True)
    sum_two = jnp.sum(scaled, 0, keepdims=True)
    bias_pair[0] = jnp.concatenate(
        [sum_one, sum_two, jnp.zeros((6, hidden_width), F32)], 0
    )
    go(remote(bias_pair.at[0], bias_pair.at[1], bp_sem.at[0], bp_sem.at[1], feat=mate))
    mixed = (dot_nn(matrix_two, hidden) * inverse_two).astype(BF16)
    flat_two[0:hidden_width] = dot_tn(hidden[:seeds], scaled_low)
    for r in range(relations):
        flat_two[(r + 1) * hidden_width : (r + 2) * hidden_width] = dot_tn(
            mixed[r * seeds : (r + 1) * seeds], scaled_plane
        )

    def share(q):
        return pl.ds(pl.multiple_of(q * share_two, 8), share_two)

    for j in range(half):
        q = 2 * j + 1 - parity
        go(remote(flat_two.at[share(q)], pair_two.at[j], p_send.at[j], p_recv.at[j], feat=mate))

    fetch_x.wait()
    fetch_words.wait()
    base = lax.broadcasted_iota(jnp.int32, (1, rows), 1) // words_one
    floor = jnp.left_shift(jnp.ones_like(base), base).astype(F32)

    def gather(b, unused):
        x = x_ref[b]
        panels[b, 0:columns] = dot_nt(x[:, :rows], order_ref[...]).astype(BF16)
        probe = jnp.concatenate([x, jnp.ones((16, nodes), BF16)], 0)
        for r in range(relations):
            words = words_ref[b, r]
            matrix = jnp.concatenate(
                [jnp.bitwise_and(words, 1 << k).astype(F32).astype(BF16) for k in range(BITS)], 0
            )
            product = dot_nt(probe, matrix)
            inverse = 1.0 / jnp.maximum(product[columns : columns + 1], floor)
            panels[b, (r + 1) * columns : (r + 2) * columns] = (
                product[:columns] * inverse
            ).astype(BF16)
        return unused

    first, second = batches // 4, 5 * batches // 8
    lax.fori_loop(0, first, gather, 0)

    for j in range(half):
        remote(pair_two.at[j], pair_two.at[j], p_send.at[j], p_recv.at[j], feat=mate).wait_recv()
        both = flat_two[share(2 * j + parity)] + pair_two[j]
        for i in range(reps):
            mine_two[i, j] = both[i * part_two : (i + 1) * part_two]
    for t in range(1, reps):
        i = rep_peer(t)
        send_two[i] = mine_two[i].astype(BF16)
        go(remote(send_two.at[i], rep_two.at[my_rep], r_send.at[t], r_recv.at[my_rep], rep=i))
    remote(bias_pair.at[0], bias_pair.at[1], bp_sem.at[0], bp_sem.at[1], feat=mate).wait_recv()
    bias_feat[place] = bias_pair[0] + bias_pair[1]
    for t in range(1, half):
        go(remote(bias_feat.at[place], bias_feat.at[place], bs_send.at[t], bs_recv.at[place], feat=peer(t)))

    lax.fori_loop(first, second, gather, 0)

    for t in range(1, half):
        p = lax.rem(me + feats - 2 * t, feats)
        remote(hbuf.at[p], hbuf.at[p], h_send.at[t], h_recv.at[p], feat=mate).wait_recv()
        go(remote(hbuf.at[p], hbuf.at[p], h_fwd.at[t], h_recv.at[p], feat=mate))

    lax.fori_loop(second, batches, gather, 0)

    for t in range(1, half):
        j = lax.rem(place + half - t, half)
        remote(bias_feat.at[j], bias_feat.at[j], bs_send.at[t], bs_recv.at[j], feat=mate).wait_recv()
    sum_feat = bias_feat[0]
    for j in range(1, half):
        sum_feat = sum_feat + bias_feat[j]
    bias_rep[my_rep] = sum_feat
    for t in range(1, reps):
        go(remote(bias_rep.at[my_rep], bias_rep.at[my_rep], br_send.at[t], br_recv.at[my_rep], rep=rep_peer(t)))

    for t in range(half):
        p = lax.rem(mate + feats - 2 * t, feats)
        remote(hbuf.at[p], hbuf.at[p], h_send.at[0], h_recv.at[p], feat=mate).wait_recv()

    acc_one[...] = dot_nn(panels[0], hbuf[0])

    def panel(b, unused):
        acc_one[...] += dot_nn(panels[b], hbuf[b])
        return unused

    lax.fori_loop(1, batches, panel, 0)

    def rows_of(i):
        return pl.ds(pl.multiple_of(i * share_one, 8), share_one)

    for t in range(1, reps):
        i = rep_peer(t)
        wire_one[i] = acc_one[rows_of(i)].astype(BF16)
        go(remote(wire_one.at[i], land_one.at[my_rep], a_send.at[t], a_recv.at[my_rep], rep=i))

    group_two[...] = mine_two[my_rep]
    for t in range(1, reps):
        i = lax.rem(my_rep + reps - t, reps)
        remote(rep_two.at[i], rep_two.at[i], r_send.at[t], r_recv.at[i], rep=i).wait_recv()
        group_two[...] += rep_two[i].astype(F32)
    for t in range(1, half):
        q = peer(t)
        wire_two[q // 2] = group_two[q // 2].astype(BF16)
        go(remote(wire_two.at[q // 2], land_two.at[place], s_send.at[t], s_recv.at[place], feat=q))
    whole_two = group_two[place]
    for t in range(1, half):
        j = lax.rem(place + half - t, half)
        remote(land_two.at[j], land_two.at[j], s_send.at[t], s_recv.at[j], feat=mate).wait_recv()
        whole_two = whole_two + land_two[j].astype(F32)
    out_two[me, my_rep] = whole_two.astype(BF16)
    for t in range(1, reps):
        go(remote(out_two.at[me, my_rep], out_two.at[me, my_rep], z_send.at[t], z_recv.at[my_rep], rep=rep_peer(t)))

    whole_one = acc_one[rows_of(my_rep)]
    for t in range(1, reps):
        i = lax.rem(my_rep + reps - t, reps)
        remote(land_one.at[i], land_one.at[i], a_send.at[t], a_recv.at[i], rep=i).wait_recv()
        whole_one = whole_one + land_one[i].astype(F32)
    out_one[my_rep] = whole_one.astype(BF16)
    for t in range(1, reps):
        go(remote(out_one.at[my_rep], out_one.at[my_rep], c_send.at[t], c_recv.at[my_rep], rep=rep_peer(t)))

    for t in range(1, reps):
        i = lax.rem(my_rep + reps - t, reps)
        remote(out_two.at[me, i], out_two.at[me, i], z_send.at[t], z_recv.at[i], rep=i).wait_recv()
    for t in range(1, half):
        go(remote(out_two.at[me], out_two.at[me], g_send.at[t], g_recv.at[me], feat=peer(t)))
    go(remote(out_two.at[me], out_two.at[me], g_send.at[0], g_recv.at[me], feat=mate))
    for t in range(1, reps):
        i = lax.rem(my_rep + reps - t, reps)
        remote(bias_rep.at[i], bias_rep.at[i], br_send.at[t], br_recv.at[i], rep=i).wait_recv()
    sum_rep = bias_rep[0]
    for i in range(1, reps):
        sum_rep = sum_rep + bias_rep[i]
    out_bias[...] = sum_rep

    for t in range(1, half):
        p = lax.rem(me + feats - 2 * t, feats)
        remote(out_two.at[p], out_two.at[p], g_send.at[t], g_recv.at[p], feat=mate).wait_recv()
        go(remote(out_two.at[p], out_two.at[p], g_fwd.at[t], g_recv.at[p], feat=mate))
    for t in range(half):
        p = lax.rem(mate + feats - 2 * t, feats)
        remote(out_two.at[p], out_two.at[p], g_send.at[0], g_recv.at[p], feat=mate).wait_recv()
    for t in range(1, reps):
        i = lax.rem(my_rep + reps - t, reps)
        remote(out_one.at[i], out_one.at[i], c_send.at[t], c_recv.at[i], rep=i).wait_recv()
    for copy in pending:
        copy.wait_send()


def widen(one_ref, two_ref, bias_ref, wide_one, wide_two, first, second):
    wide_one[...] = one_ref[...].astype(F32)
    wide_two[...] = two_ref[...].astype(F32)
    first[...] = bias_ref[0]
    second[...] = bias_ref[1]


def on_device(features, adjacency_one, pre_hidden, adjacency_two, weight_two, out_grad):
    feats, reps = lax.axis_size("feat"), lax.axis_size("rep")
    half = feats // 2
    seeds = out_grad.shape[2]
    factor = float(seeds * feats * reps) ** (-0.5)
    x, words = features[0], adjacency_one[0]
    batches, columns, nodes = x.shape
    relations = words.shape[1]
    rows, width = pre_hidden.shape[2:]
    share_one = (relations + 1) * columns // reps
    share_two = (relations + 1) * width // feats
    vmem = pl.BlockSpec(memory_space=pltpu.VMEM)
    hbm = pl.BlockSpec(memory_space=pl.ANY)
    dma = pltpu.SemaphoreType.DMA
    one, two, bias = pl.pallas_call(
        functools.partial(kernel, feats, reps, factor),
        out_shape=(
            jax.ShapeDtypeStruct((reps, share_one, width), BF16),
            jax.ShapeDtypeStruct((feats, reps, share_two // reps, width), BF16),
            jax.ShapeDtypeStruct((8, width), F32),
        ),
        in_specs=[hbm, hbm, vmem, vmem, hbm, vmem],
        out_specs=(vmem, vmem, vmem),
        scratch_shapes=[
            pltpu.VMEM(x.shape, BF16),
            pltpu.VMEM(words.shape, jnp.int32),
            pltpu.VMEM(weight_two.shape, BF16),
            pltpu.VMEM((batches, (relations + 1) * columns, rows), BF16),
            pltpu.VMEM((feats, rows, width), BF16),
            pltpu.VMEM((rows, rows), BF16),
            pltpu.VMEM(((relations + 1) * columns, width), F32),
            pltpu.VMEM((reps, share_one, width), BF16),
            pltpu.VMEM((reps, share_one, width), BF16),
            pltpu.VMEM(((relations + 1) * width, width), F32),
            pltpu.VMEM((half, share_two, width), F32),
            pltpu.VMEM((half, share_two // reps, width), BF16),
            pltpu.VMEM((half, share_two // reps, width), BF16),
            pltpu.VMEM((reps, half, share_two // reps, width), F32),
            pltpu.VMEM((reps, half, share_two // reps, width), BF16),
            pltpu.VMEM((reps, half, share_two // reps, width), BF16),
            pltpu.VMEM((half, share_two // reps, width), F32),
            pltpu.VMEM((2, 8, width), F32),
            pltpu.VMEM((half, 8, width), F32),
            pltpu.VMEM((reps, 8, width), F32),
            dma((3,)), dma((half,)), dma((half,)), dma((feats,)),
            dma((half,)), dma((half,)), dma((half,)), dma((half,)),
            dma((reps,)), dma((reps,)), dma((reps,)), dma((reps,)), dma((half,)), dma((half,)), dma((feats,)),
            dma((reps,)), dma((reps,)), dma((reps,)), dma((reps,)),
            dma((2,)), dma((half,)), dma((half,)), dma((reps,)), dma((reps,)),
        ],
        compiler_params=pltpu.CompilerParams(collective_id=0, has_side_effects=True),
    )(x, words, pre_hidden[0, 0], adjacency_two[0, 0], weight_two, out_grad[0, 0])
    count = relations + 1
    group = 3 if count % 3 == 0 else 1

    def block(height):
        return pl.BlockSpec((group, height, width), lambda i: (i, 0, 0))

    line = pl.BlockSpec((width,), lambda i: (0,))
    grad_w1, grad_w2, grad_b1, grad_b2 = pl.pallas_call(
        widen,
        grid=(count // group,),
        out_shape=(
            jax.ShapeDtypeStruct((count, columns, width), F32),
            jax.ShapeDtypeStruct((count, width, width), F32),
            jax.ShapeDtypeStruct((width,), F32),
            jax.ShapeDtypeStruct((width,), F32),
        ),
        in_specs=[block(columns), block(width), pl.BlockSpec((8, width), lambda i: (0, 0))],
        out_specs=(block(columns), block(width), line, line),
    )(one.reshape(count, columns, width), two.reshape(count, width, width), bias)
    return (grad_w1, grad_b1, grad_w2, grad_b2)


def solution(mesh):
    placed = (
        P("rep", None, "feat", None),
        P("rep", None, None, None, None),
        P("rep", "feat", None, None),
        P("rep", "feat", None, None, None),
        P(),
        P("rep", "feat", None, None),
    )
    return jax.shard_map(
        on_device,
        mesh=mesh,
        in_specs=placed,
        out_specs=(P(None, "feat", None), P(), P(), P()),
        check_vma=False,
    )
```

profile of v0, /device:TPU:27, one launch (start us, length us, event | category | flops | bytes accessed | tf_op | source)
XLA Modules:
  0.0 44.1 jit_solution(13772637737720001596)
XLA Ops:
  0.6 40.8 %shard_map.93 = (bf16[4,192,256]{2,1,0:T(8,128)(2,1)}, bf16[8,4,48,256]{3,2,1,0:T(8,128)(2,1)}, f32[8,256]{1,0:T(8,128)}) custom-call(bf16[8,128,512]{2,1,0:T(8,128)(2,1)} %bitcast.8, s32[8,5,16,512]{3,2,1,0:T(8,128)} %bitcast.7, bf16[256,256]{1,0:T(8,128)(2,1)} %bitcast.11, s32[5,8,256]{2,1,0:T(8,128)} %bitcast.13, bf16[6,256,256]{2,1,0:T(8,128)(2,1)} %weight_hbm.1, ...), custom_call_target="tpu_custom_call" | custom-call | tf_op jit(solution)/shard_map/pallas_call | solution.py:301
  41.5 2.6 %shard_map.94 = (f32[6,128,256]{2,1,0:T(8,128)}, f32[6,256,256]{2,1,0:T(8,128)}, f32[256]{0:T(256)}, f32[256]{0:T(256)}) custom-call(bf16[6,128,256]{2,1,0:T(8,128)(2,1)} %bitcast.10, bf16[6,256,256]{2,1,0:T(8,128)(2,1)} %bitcast.9, f32[8,256]{1,0:T(8,128)} %get-tuple-element.13.bias_ref), custom_call_target="tpu_custom_call" | custom-call | tf_op jit(solution)/shard_map/pallas_call | solution.py:346
where the time goes:
time: 44.3 us; the launch traced here: 44.1 us
  Pallas kernels  43.4 us (98%)
  between operations  0.64 us (1%)
    pallas_call x1, Pallas kernels, on_device(): pl.pallas_call(functools.partial(kernel, feats, reps, factor), out_shape=...  40.8 us
    pallas_call x1, Pallas kernels, on_device(): pl.pallas_call(widen, grid=(count // group,), out_shape=(jax.ShapeDtypeSt...  2.58 us

commit v1 on v0

--- a/solution.py
+++ b/solution.py
@@ -301,9 +301,9 @@
     one, two, bias = pl.pallas_call(
         functools.partial(kernel, feats, reps, factor),
         out_shape=(
-            jax.ShapeDtypeStruct((reps, share_one, width), BF16),
-            jax.ShapeDtypeStruct((feats, reps, share_two // reps, width), BF16),
-            jax.ShapeDtypeStruct((8, width), F32),
+            pltpu.VMEM((reps, share_one, width), BF16),
+            pltpu.VMEM((feats, reps, share_two // reps, width), BF16),
+            pltpu.VMEM((8, width), F32),
         ),
         in_specs=[hbm, hbm, vmem, vmem, hbm, vmem],
         out_specs=(vmem, vmem, vmem),
@@ -334,7 +334,7 @@
             dma((reps,)), dma((reps,)), dma((reps,)), dma((reps,)),
             dma((2,)), dma((half,)), dma((half,)), dma((reps,)), dma((reps,)),
         ],
-        compiler_params=pltpu.CompilerParams(collective_id=0, has_side_effects=True),
+        compiler_params=pltpu.CompilerParams(collective_id=0, has_side_effects=True, vmem_limit_bytes=60*2**20),
     )(x, words, pre_hidden[0, 0], adjacency_two[0, 0], weight_two, out_grad[0, 0])
     count = relations + 1
     group = 3 if count % 3 == 0 else 1
@@ -354,6 +354,7 @@
         ),
         in_specs=[block(columns), block(width), pl.BlockSpec((8, width), lambda i: (0, 0))],
         out_specs=(block(columns), block(width), line, line),
+        compiler_params=pltpu.CompilerParams(vmem_limit_bytes=24 * 2**20),
     )(one.reshape(count, columns, width), two.reshape(count, width, width), bias)
     return (grad_w1, grad_b1, grad_w2, grad_b2)
 

time: 44.3 us -> 42.1 us (0.950)
  Pallas kernels: 43.4 us -> 41.3 us
    pallas_call x1, Pallas kernels: 2.58 us -> 1.49 us  [on_device(): pl.pallas_call(widen, grid=(count // group,), out_shape=(jax.ShapeDtypeSt...]
    pallas_call x1, Pallas kernels: 40.8 us -> 39.8 us  [on_device(): pl.pallas_call(functools.partial(kernel, feats, reps, factor), out_shape=...]
where the time goes in v1:
time: 42.1 us; the launch traced here: 42 us
  Pallas kernels  41.3 us (98%)
  between operations  0.64 us (2%)
    pallas_call x1, Pallas kernels, on_device(): pl.pallas_call(functools.partial(kernel, feats, reps, factor), out_shape=...  39.8 us
    pallas_call x1, Pallas kernels, on_device(): pl.pallas_call(widen, grid=(count // group,), out_shape=(jax.ShapeDtypeSt...  1.49 us

profile of v1, /device:TPU:27, one launch (start us, length us, event | category | flops | bytes accessed | tf_op | source)
XLA Modules:
  0.0 42.0 jit_solution(15515748459503588211)
XLA Ops:
  0.6 39.8 %shard_map.93 = (bf16[4,192,256]{2,1,0:T(8,128)(2,1)S(1)}, bf16[8,4,48,256]{3,2,1,0:T(8,128)(2,1)S(1)}, f32[8,256]{1,0:T(8,128)S(1)}) custom-call(bf16[8,128,512]{2,1,0:T(8,128)(2,1)} %bitcast.10, s32[8,5,16,512]{3,2,1,0:T(8,128)} %bitcast.9, bf16[256,256]{1,0:T(8,128)(2,1)} %bitcast.11, s32[5,8,256]{2,1,0:T(8,128)} %bitcast.13, ...), custom_call_target="tpu_custom_call" | custom-call | tf_op jit(solution)/shard_map/pallas_call | solution.py:301
  40.5 1.5 %shard_map.94 = (f32[6,128,256]{2,1,0:T(8,128)}, f32[6,256,256]{2,1,0:T(8,128)}, f32[256]{0:T(256)}, f32[256]{0:T(256)}) custom-call(bf16[6,128,256]{2,1,0:T(8,128)(2,1)S(1)} %bitcast.8, bf16[6,256,256]{2,1,0:T(8,128)(2,1)S(1)} %bitcast.7, f32[8,256]{1,0:T(8,128)S(1)} %get-tuple-element.13.bias_ref), custom_call_target="tpu_custom_call" | custom-call | tf_op jit(solution)/shard_map/pallas_call | solution.py:346
